TPU v7x, 32 devices: a whole 2x2x4 slice. The times are simulated.
32 devices in a mesh: dp: 16 (over z, y, core), level: 2 (over x).
Axes of the slice: x: 2, y: 2, z: 4, core: 2. Of those that a mesh axis runs over, the one named last changes fastest.
Arguments:
- token_ids: int32 [16, 2, 1536], P('dp', 'level'), may hold values from 0 to 1023
- decoded_mask: int32 [16, 2, 1536], P('dp', 'level'), may hold values 0 or 1
- levels_done: int32 [16], P('dp'), may hold values from 0 to 1
- code_tables: bfloat16 [2, 1024, 1024], P('level'), may hold values from -6 to 6
- mask_vectors: bfloat16 [2, 1024], P('level'), may hold values from -6 to 6
- w_qkv: bfloat16 [3, 1024, 1024], P(None, 'dp', 'level'), may hold values from -6 to 6
- w_out: bfloat16 [1024, 1024], P('level', 'dp'), may hold values from -0.1875 to 0.1875
- w_expand: bfloat16 [1024, 2048], P('dp'), may hold values from -0.1875 to 0.1875
- w_depth: bfloat16 [5, 1024], replicated, may hold values from -2.5 to 2.5
- w_project: bfloat16 [1024, 1024], P('dp'), may hold values from -0.1875 to 0.1875
- level_heads: bfloat16 [2, 1024, 1024], P('level'), may hold values from -0.1875 to 0.1875
Outputs:
- logits: bfloat16 [16, 2, 1536, 1024], P('dp', 'level')
Inputs may be any that keep to these rules, and one draw needn't show every extreme that they name: `levels_done`: levels below it are fully decoded; the level equal to it is the one being decoded.
All inputs are finite; a program needn't handle non-finite values. No bound on the sum of `decoded_mask` on one device may be relied on, other than what follows from the above.
Results may differ from a plain program's by a relative error of at most 0.006.
Values may be sent and summed in bfloat16 or wider, within the bound.
A program may use at most 192 MiB of HBM per device.

v0:
```python
import jax
import jax.numpy as jnp
from jax import lax
from jax.sharding import PartitionSpec as P

HEADS = 16


def with_halo(x, sides, width):
    for axis, dim in sides:
        devices, length = (lax.axis_size(axis), x.shape[dim])
        up = [(i, (i + 1) % devices) for i in range(devices - 1)]
        down = [(j, i) for i, j in up]
        last = lax.slice_in_dim(x, length - width, length, axis=dim)
        leading = lax.slice_in_dim(x, 0, width, axis=dim)
        before = lax.ppermute(last, axis, up)
        after = lax.ppermute(leading, axis, down)
        x = jnp.concatenate([before, x, after], axis=dim)
    return x


def layer_norm(values):
    centered = values - jnp.mean(values, axis=-1, keepdims=True)
    variance = jnp.mean(centered * centered, axis=-1, keepdims=True)
    return centered * lax.rsqrt(variance + 1e-05)


def contract_with(left, shard_piece):
    return jnp.dot(left, shard_piece, preferred_element_type=jnp.float32)


def contract_three(left, shard_piece):
    return jnp.einsum("fk,jkc->jfc", left, shard_piece, preferred_element_type=jnp.float32)


def body(
    token_ids,
    decoded_mask,
    levels_done,
    code_tables,
    mask_vectors,
    w_qkv,
    w_out,
    w_expand,
    w_depth,
    w_project,
    level_heads,
):
    frames = token_ids.shape[2]
    model_width = code_tables.shape[2]
    groups = lax.axis_size("level")
    level_index = lax.axis_index("level")
    local_rows = frames // groups
    head_dim = model_width // HEADS
    scale = head_dim ** (-0.5)
    id_row = token_ids[0, 0]
    flag_row = decoded_mask[0, 0]
    done_count = levels_done[0]
    own_table = code_tables[0]
    fill_row = mask_vectors[0].astype(jnp.float32)
    all_live = level_index < done_count
    current = level_index == done_count
    use_token = all_live | current & (flag_row == 1)
    codes = lax.broadcasted_iota(jnp.int32, (frames, own_table.shape[0]), 1)
    onehot = (id_row[:, None] == codes).astype(jnp.bfloat16)
    picked = jnp.dot(onehot, own_table, preferred_element_type=jnp.float32)
    level_terms = (
        jnp.where(use_token[:, None], picked, fill_row[None, :])
        .astype(jnp.bfloat16)
        .reshape(groups, local_rows, model_width)
    )
    received = lax.all_to_all(level_terms, "level", split_axis=0, concat_axis=0, tiled=True)
    own_rows = jnp.sum(received, axis=0, dtype=jnp.float32)
    normed = layer_norm(own_rows).astype(jnp.bfloat16)
    full_columns = lax.all_gather(w_qkv, "level", axis=2, tiled=True)
    projected = contract_three(
        normed, lax.all_gather(full_columns, "dp", axis=1, tiled=True)
    ).astype(jnp.bfloat16)
    queries = projected[0].reshape(local_rows, HEADS, head_dim)
    running_max = jnp.full((HEADS, local_rows), -1e30, jnp.float32)
    accumulated = jnp.zeros((local_rows, HEADS, head_dim), jnp.float32)
    key_piece = lax.all_gather(projected[1], "level", axis=0, tiled=True)
    value_piece = lax.all_gather(projected[2], "level", axis=0, tiled=True)
    piece_rows = key_piece.shape[0]
    key_three = key_piece.reshape(piece_rows, HEADS, head_dim)
    value_three = value_piece.reshape(piece_rows, HEADS, head_dim)
    scores = (
        jnp.einsum("qhd,khd->hqk", queries, key_three, preferred_element_type=jnp.float32) * scale
    )
    new_max = jnp.maximum(running_max, jnp.max(scores, axis=-1))
    shrink = jnp.exp(running_max - new_max)
    weights = jnp.exp(scores - new_max[:, :, None])
    weight_sum = jnp.sum(weights, axis=-1)
    added = jnp.einsum(
        "hqk,khd->qhd",
        weights.astype(jnp.bfloat16),
        value_three,
        preferred_element_type=jnp.float32,
    )
    accumulated = accumulated * shrink.T[:, :, None] + added
    running_max, weight_sum, accumulated = (new_max, weight_sum, accumulated)
    attended = (
        (accumulated / weight_sum.T[:, :, None])
        .reshape(local_rows, model_width)
        .astype(jnp.bfloat16)
    )
    out_full = lax.all_gather(w_out, "level", axis=0, tiled=True)
    after_attn = own_rows + jnp.dot(
        attended,
        lax.all_gather(out_full, "dp", axis=1, tiled=True),
        preferred_element_type=jnp.float32,
    )
    normed_two = layer_norm(after_attn).astype(jnp.bfloat16)
    gate_linear = contract_with(normed_two, lax.all_gather(w_expand, "dp", axis=0, tiled=True))
    gated = (gate_linear[:, :model_width] * jax.nn.sigmoid(gate_linear[:, model_width:])).astype(
        jnp.bfloat16
    )
    half_width = w_depth.shape[0] // 2
    padded = with_halo(gated, (("level", 0),), half_width)
    conv = jnp.zeros((local_rows, model_width), jnp.float32)
    for tap_index in range(w_depth.shape[0]):
        conv = conv + padded[tap_index : tap_index + local_rows].astype(jnp.float32) * w_depth[
            tap_index
        ].astype(jnp.float32)
    activated = (conv * jax.nn.sigmoid(conv)).astype(jnp.bfloat16)
    after_conv = after_attn + contract_with(
        activated, lax.all_gather(w_project, "dp", axis=0, tiled=True)
    )
    final_norm = layer_norm(after_conv).astype(jnp.bfloat16)
    own_head = level_heads[0]
    logits = jnp.dot(
        lax.all_gather(final_norm, "level", axis=0, tiled=True),
        own_head,
        preferred_element_type=jnp.float32,
    ).astype(jnp.bfloat16)
    return logits[None, None]


def solution(mesh):
    return jax.shard_map(
        body,
        mesh=mesh,
        in_specs=(
            P("dp", "level", None),
            P("dp", "level", None),
            P("dp"),
            P("level", None, None),
            P("level", None),
            P(None, "dp", "level"),
            P("level", "dp"),
            P("dp", None),
            P(),
            P("dp", None),
            P("level", None, None),
        ),
        out_specs=P("dp", "level", None, None),
        check_vma=False,
    )
```

profile of v0, /device:TPU:0, one launch (start us, length us, event | category | flops | bytes accessed | tf_op | source)
XLA Modules:
  0.0 386.5 jit_solution(2967878390888933590)
XLA Ops:
  6.5 10.6 %all_gather.27 = bf16[3,64,1024]{2,1,0:T(8,128)(2,1)} all-gather(bf16[3,64,512]{2,1,0:T(8,128)(2,1)} %param.16), channel_id=1, replica_groups=mesh['dp'=16,'level'=2] {'level'}, dimensions={2}, use_global_device_ids=true | all-gather | bytes 589824 | tf_op jit(solution)/shard_map/all_gather | solution.py:75
  17.1 0.0 all-gather.10.cloned.1.call-update
  17.2 0.0 all-gather.20.cloned.1.call-start
  17.9 0.7 broadcast_in_dim.53
  18.5 0.7 reduce.2
  19.3 0.7 or_reduce_fusion
  20.0 4.3 %select_convert_fusion = bf16[1536,1024]{1,0:T(8,128)(2,1)S(1)} fusion(f32[1024]{0:T(1024)S(1)} %bitcast.56, s32[1536]{0:T(1024)S(1)} %reduce.2, pred[1536]{0:T(1024)(128)(4,1)S(1)} %or_reduce_fusion, bf16[1,1024,1024]{2,1,0:T(8,128)(2,1)S(1)} %copy-done), kind=kOutput, calls=%fused_computation.7 | convolution fusion | flops 3224371200 | bytes 5254656 | tf_op jit(solution)/shard_map/dot_general | solution.py:66
  24.3 38.4 %all_to_all.5 = bf16[2,768,1024]{2,1,0:T(8,128)(2,1)S(1)} all-to-all(bf16[2,768,1024]{2,1,0:T(8,128)(2,1)S(1)} %bitcast.48), channel_id=1, replica_groups=mesh['dp'=16,'level'=2] {'level'}, dimensions={0} | all-to-all | bytes 6291456 | tf_op jit(solution)/shard_map/all_to_all | solution.py:72
  62.7 0.7 convert_reduce_fusion
  63.4 0.4 multiply_reduce_fusion.3
  63.8 15.3 %all-gather.10.cloned.1.call-done = bf16[3,1024,1024]{2,1,0:T(8,128)(2,1)} async-done(((bf16[3,64,1024]{2,1,0:T(8,128)(2,1)}), bf16[3,1024,1024]{2,1,0:T(8,128)(2,1)}) %all-gather.10.cloned.1.call-update) | async-done | bytes 6291472 | tf_op jit(solution)/shard_map/all_gather | solution.py:77
  79.1 8.3 %convert_bitcast_fusion = bf16[3,768,1024]{2,1,0:T(8,128)(2,1)S(1)} fusion(bf16[3,1024,1024]{2,1,0:T(8,128)(2,1)} %all-gather.10.cloned.1.call-done, f32[768,1024]{1,0:T(8,128)S(1)} %get-tuple-element.6, f32[768]{0:T(1024)S(1)} %add_rsqrt_fusion.2, f32[768]{0:T(1024)S(1)} %broadcast_multiply_fusion.2), kind=kOutput, calls=%fused_computation.10 | convolution fusion | flops 4836556800 | bytes 14161920 | tf_op jit(solution)/shard_map/fk,jkc->jfc/dot_general | solution.py:33
  87.4 2.3 fusion.36
  89.6 0.0 all-gather.20.cloned.1.call-update
  89.7 0.0 all-gather.22.cloned.1.call-start
  89.7 0.7 all-gather.22.cloned.1.call-update
  90.4 0.0 all-gather.12.cloned.1.call-start
  90.4 0.0 copy-done.5
  90.5 5.0 %all_gather.31 = bf16[1024,64]{0,1:T(8,128)(2,1)} all-gather(bf16[512,64]{0,1:T(8,128)(2,1)S(1)} %copy-done.5), channel_id=1, replica_groups=mesh['dp'=16,'level'=2] {'level'}, dimensions={0}, use_global_device_ids=true | all-gather | bytes 196608 | tf_op jit(solution)/shard_map/all_gather | solution.py:107
  95.5 0.0 all-gather.12.cloned.1.call-update
  95.5 0.0 all-gather.14.cloned.1.call-start
  95.6 0.5 all-gather.14.cloned.1.call-update
  96.1 0.0 all-gather.16.cloned.1.call-start
  96.2 0.5 all-gather.16.cloned.1.call-update
  96.7 0.2 all-gather.18.cloned.1.call-start
  96.9 1.6 copy.15
  98.5 34.9 %all-gather.20.cloned.1.call-done = bf16[1,1536,1024]{2,1,0:T(8,128)(2,1)} async-done(((bf16[1,768,1024]{2,1,0:T(8,128)(2,1)}), bf16[1,1536,1024]{2,1,0:T(8,128)(2,1)}) %all-gather.20.cloned.1.call-update) | async-done | bytes 3145744 | tf_op jit(solution)/shard_map/all_gather | solution.py:82
  133.4 3.2 copy.16
  136.6 28.8 %multiply_reduce_fusion = (f32[16,768]{1,0:T(8,128)S(1)}, f32[16,768,1536]{2,1,0:T(8,128)}) fusion(bf16[768,16,64]{0,2,1:T(8,128)(2,1)} %bitcast.47, bf16[1536,16,64]{0,2,1:T(8,128)(2,1)S(1)} %bitcast.45), kind=kOutput, calls=%fused_computation.1 | convolution fusion | flops 2453655552 | bytes 80265216 | tf_op jit(solution)/shard_map/qhd,khd->hqk/dot_general | solution.py:88
  165.4 24.1 %fusion = f32[16,768]{1,0:T(8,128)S(1)} fusion(f32[16,768,1536]{2,1,0:T(8,128)} %get-tuple-element.20, f32[16,768]{1,0:T(8,128)S(1)} %get-tuple-element.13), kind=kLoop, calls=%fused_computation.2 | loop fusion | flops 56610816 | bytes 75595776 | tf_op jit(solution)/shard_map/reduce_sum | solution.py:93
  189.5 0.0 all-gather.22.cloned.1.call-done
  189.5 3.2 copy.17
  192.7 27.7 %fusion.11 = bf16[768,16,64]{0,2,1:T(8,128)(2,1)} fusion(bf16[1536,16,64]{0,2,1:T(8,128)(2,1)S(1)} %bitcast.46, f32[16,768,1536]{2,1,0:T(8,128)} %get-tuple-element.20, f32[16,768]{1,0:T(8,128)S(1)} %get-tuple-element.13, f32[768,16]{0,1:T(8,128)S(1)} %bitcast.50, f32[768,16]{0,1:T(8,128)S(1)} %get-tuple-element.12), kind=kOutput, calls=%fused_computation.20 | convolution fusion | flops 2474901504 | bytes 80363520 | tf_op jit(solution)/shard_map/hqk,khd->qhd/dot_general | solution.py:94
  220.4 3.0 all-gather.12.cloned.1.call-done
  223.4 4.9 %fusion.38 = (f32[768]{0:T(1024)S(1)}, f32[768,1024]{1,0:T(8,128)S(1)}) fusion(f32[768,1024]{1,0:T(8,128)} %copy-done.2, bf16[768,1024]{0,1:T(8,128)(2,1)} %bitcast.49, bf16[1024,1024]{0,1:T(8,128)(2,1)} %all-gather.12.cloned.1.call-done), kind=kOutput, calls=%fused_computation.73 | convolution fusion | flops 1612184832 | bytes 9964544 | tf_op jit(solution)/shard_map/dot_general | solution.py:108
  228.3 0.4 multiply_reduce_fusion.2
  228.8 45.8 %all-gather.14.cloned.1.call-done = bf16[1024,2048]{1,0:T(8,128)(2,1)} async-done(((bf16[64,2048]{1,0:T(8,128)(2,1)}), bf16[1024,2048]{1,0:T(8,128)(2,1)}) %all-gather.14.cloned.1.call-update) | async-done | bytes 4194320 | tf_op jit(solution)/shard_map/all_gather | solution.py:114
  274.6 5.3 %fusion.22 = f32[768,2048]{1,0:T(8,128)S(1)} fusion(bf16[1024,2048]{1,0:T(8,128)(2,1)} %all-gather.14.cloned.1.call-done, f32[768,1024]{1,0:T(8,128)S(1)} %get-tuple-element.22, f32[768]{0:T(1024)S(1)} %add_rsqrt_fusion.1, f32[768]{0:T(1024)S(1)} %broadcast_multiply_fusion.1), kind=kOutput, calls=%fused_computation.41 | convolution fusion | flops 3223584768 | bytes 13637632 | tf_op jit(solution)/shard_map/dot_general | solution.py:29
  279.9 0.9 fusion.13
  280.8 1.1 copy-done.4
  281.9 3.4 collective-permute-start
  285.3 1.5 collective-permute-start.1
  286.9 29.7 %all-gather.16.cloned.1.call-done = bf16[1024,1024]{1,0:T(8,128)(2,1)} async-done(((bf16[64,1024]{1,0:T(8,128)(2,1)}), bf16[1024,1024]{1,0:T(8,128)(2,1)}) %all-gather.16.cloned.1.call-update) | async-done | bytes 2097168 | tf_op jit(solution)/shard_map/all_gather | solution.py:127
  316.6 9.5 %fusion.39 = (f32[768]{0:T(1024)S(1)}, f32[768,1024]{1,0:T(8,128)S(1)}) fusion(f32[768,1024]{1,0:T(8,128)S(1)} %get-tuple-element.22, bf16[1024,1024]{1,0:T(8,128)(2,1)} %all-gather.16.cloned.1.call-done, bf16[768,1024]{1,0:T(8,128)(2,1)} %copy-done.4, bf16[2,1024]{1,0:T(2,128)(2,1)S(1)} %collective-permute-done.1, ...), kind=kOutput, calls=%fused_computation.74 | convolution fusion | flops 1636564224 | bytes 9993216 | tf_op jit(solution)/shard_map/dot_general | solution.py:29
  326.1 0.4 multiply_reduce_fusion.1
  326.6 1.5 multiply_convert_fusion
  328.1 43.8 %all-gather.18.cloned.1.call-done = bf16[1536,1024]{1,0:T(8,128)(2,1)} async-done(((bf16[768,1024]{1,0:T(8,128)(2,1)}), bf16[1536,1024]{1,0:T(8,128)(2,1)}) %all-gather.18.cloned.1.call-update) | async-done | bytes 3145744 | tf_op jit(solution)/shard_map/all_gather | solution.py:132
  371.9 7.8 %fusion.5 = bf16[1,1,1536,1024]{3,2,1,0:T(8,128)(2,1)} fusion(bf16[1536,1024]{1,0:T(8,128)(2,1)} %all-gather.18.cloned.1.call-done, bf16[1,1024,1024]{2,1,0:T(8,128)(2,1)} %param.21), kind=kOutput, calls=%fused_computation.12 | convolution fusion | flops 3222798336 | bytes 8388608 | tf_op jit(solution)/shard_map/dot_general | solution.py:131
  (25 shorter events, 0.1 us)
Async XLA Ops:
  6.5 13.5 %copy-start = (bf16[1,1024,1024]{2,1,0:T(8,128)(2,1)S(1)}, bf16[1,1024,1024]{2,1,0:T(8,128)(2,1)}, u32[]{:S(2)}) copy-start(bf16[1,1024,1024]{2,1,0:T(8,128)(2,1)} %param.14) | copy-start | bytes 6291460
  6.5 72.5 %all-gather.10.cloned.1.call-start = ((), (), s32[]{:S(2)}) async-start(), calls=%async_computation.1 | async-start | bytes 6684672 | tf_op jit(solution)/shard_map/all_gather | solution.py:77
  17.2 116.3 %all-gather.20.cloned.1.call-start = ((), (), s32[]{:S(2)}) async-start(), calls=%async_computation.6 | async-start | bytes 4718592 | tf_op jit(solution)/shard_map/all_gather | solution.py:82
  63.3 24.0 %copy-start.2 = (f32[768,1024]{1,0:T(8,128)}, f32[768,1024]{1,0:T(8,128)S(1)}, u32[]{:S(2)}) copy-start(f32[768,1024]{1,0:T(8,128)S(1)} %get-tuple-element.6) | copy-start | bytes 9437188
  89.6 0.8 copy-start.5
  89.6 7.3 %copy-start.3 = (bf16[1,768,1024]{2,1,0:T(8,128)(2,1)S(1)}, bf16[1,768,1024]{2,1,0:T(8,128)(2,1)}, u32[]{:S(2)}) copy-start(bf16[1,768,1024]{2,1,0:T(8,128)(2,1)} %get-tuple-element.9) | copy-start | bytes 4718596
  89.7 99.8 %all-gather.22.cloned.1.call-start = ((), (), s32[]{:S(2)}) async-start(), calls=%async_computation.7 | async-start | bytes 4718592 | tf_op jit(solution)/shard_map/all_gather | solution.py:83
  90.4 133.0 %all-gather.12.cloned.1.call-start = ((), (), s32[]{:S(2)}) async-start(), calls=%async_computation.2 | async-start | bytes 2228224 | tf_op jit(solution)/shard_map/all_gather | solution.py:110
  95.5 179.1 %all-gather.14.cloned.1.call-start = ((), (), s32[]{:S(2)}) async-start(), calls=%async_computation.3 | async-start | bytes 4456448 | tf_op jit(solution)/shard_map/all_gather | solution.py:114
  96.1 220.5 %all-gather.16.cloned.1.call-start = ((), (), s32[]{:S(2)}) async-start(), calls=%async_computation.4 | async-start | bytes 2228224 | tf_op jit(solution)/shard_map/all_gather | solution.py:127
  96.7 275.2 %all-gather.18.cloned.1.call-start = ((), (), s32[]{:S(2)}) async-start(), calls=%async_computation.5 | async-start | bytes 4718592 | tf_op jit(solution)/shard_map/all_gather | solution.py:132
  279.9 6.9 %copy-start.6 = (bf16[5,1024]{1,0:T(8,128)(2,1)S(1)}, bf16[5,1024]{1,0:T(8,128)(2,1)}, u32[]{:S(2)}) copy-start(bf16[5,1024]{1,0:T(8,128)(2,1)} %param.19) | copy-start | bytes 30724
  280.8 1.1 copy-start.4
  281.9 34.7 %collective-permute-start = (bf16[2,1024]{1,0:T(2,128)(2,1)S(1)}, bf16[2,1024]{1,0:T(2,128)(2,1)S(1)}, u32[]{:S(2)}, u32[]{:S(2)}) collective-permute-start(bf16[2,1024]{1,0:T(2,128)(2,1)S(1)} %get-tuple-element.10), channel_id=1, source_target_pairs={{0,1},{2,3},{4,5},{6,7},{8,9},{10,11},{12,13},{14,15},{16,17},{18,... | collective-permute-start | bytes 12296 | tf_op jit(solution)/shard_map/ppermute | solution.py:16
  285.3 31.3 %collective-permute-start.1 = (bf16[2,1024]{1,0:T(2,128)(2,1)S(1)}, bf16[2,1024]{1,0:T(2,128)(2,1)S(1)}, u32[]{:S(2)}, u32[]{:S(2)}) collective-permute-start(bf16[2,1024]{1,0:T(2,128)(2,1)S(1)} %get-tuple-element.11), channel_id=1, source_target_pairs={{1,0},{3,2},{5,4},{7,6},{9,8},{11,10},{13,12},{15,14},{17,16},{19,... | collective-permute-start | bytes 12296 | tf_op jit(solution)/shard_map/ppermute | solution.py:17
  371.9 7.8 %copy-start.1 = (bf16[1,1024,1024]{2,1,0:T(8,128)(2,1)S(1)}, bf16[1,1024,1024]{2,1,0:T(8,128)(2,1)}, u32[]{:S(2)}) copy-start(bf16[1,1024,1024]{2,1,0:T(8,128)(2,1)} %param.14) | copy-start | bytes 6291460
Sparse Core Ops, SparseCore 0:
  17.3 61.7 all-gather.9
  89.8 43.5 all-gather.19
  135.0 44.8 all-gather.21
  181.9 41.4 all-gather.11
  225.4 49.1 all-gather.13
  276.6 39.9 all-gather.15
  328.2 43.6 all-gather.17
where the time goes:
time: 387 us
  waiting for transfers between devices  174 us (45%)
  matrix products  96.5 us (25%)
  blocking collectives  54 us (14%)
  other arithmetic  30.7 us (8%)
  between operations  14.4 us (4%)
  local copies, waits for them, and re-layouts  11.4 us (3%)
  starting transfers between devices  5.31 us (1%)
    all_gather x1, waiting for transfers between devices, body(): lax.all_gather(w_expand, 'dp', axis=0, tiled=True)  45.8 us
    all_gather x1, waiting for transfers between devices, body(): lax.all_gather(final_norm, 'level', axis=0, tiled=True)  43.8 us
    all_to_all x1, blocking collectives, body(): lax.all_to_all(level_terms, 'level', split_axis=0, concat_axis=0, tiled=T...  38.4 us
    all_gather x1, waiting for transfers between devices, body(): key_piece = lax.all_gather(projected[1], 'level', axis=0, tiled=True)  34.9 us
    all_gather x1, waiting for transfers between devices, body(): lax.all_gather(w_project, 'dp', axis=0, tiled=True)  29.7 us
    dot_general x1, matrix products, body(): jnp.einsum('qhd,khd->hqk', queries, key_three, preferred_element_type=jnp...  28.8 us
    dot_general x1, matrix products, body(): jnp.einsum('hqk,khd->qhd', weights.astype(jnp.bfloat16), value_three, pre...  27.7 us
    reduce_sum x1, other arithmetic, body(): weight_sum = jnp.sum(weights, axis=-1)  24.1 us
  transfers between devices with their start and end apart: 9, of which 6 were waited for; matrix products, arithmetic and copies ran while one was open for 28% of the time, Pallas kernels for 0%

commit v1 on v0

--- a/solution.py
+++ b/solution.py
@@ -79,7 +79,13 @@
     queries = projected[0].reshape(local_rows, HEADS, head_dim)
     running_max = jnp.full((HEADS, local_rows), -1e30, jnp.float32)
     accumulated = jnp.zeros((local_rows, HEADS, head_dim), jnp.float32)
-    key_piece = lax.all_gather(projected[1], "level", axis=0, tiled=True)
+    key_piece = jnp.roll(
+        jnp.concatenate(
+            [projected[1], lax.ppermute(projected[1], "level", [(0, 1), (1, 0)])], axis=0
+        ),
+        lax.axis_index("level") * projected[1].shape[0],
+        axis=0,
+    )
     value_piece = lax.all_gather(projected[2], "level", axis=0, tiled=True)
     piece_rows = key_piece.shape[0]
     key_three = key_piece.reshape(piece_rows, HEADS, head_dim)

time: 387 us -> 372 us (0.961)
  waiting for transfers between devices: 174 us -> 144 us
  other arithmetic: 30.7 us -> 42.9 us
    ppermute x0 -> x1, waiting for transfers between devices: none -> 64.8 us  [body(): lax.ppermute(projected[1], 'level', [(0, 1), (1, 0)])]
    all_gather x1, waiting for transfers between devices: 45.8 us -> 0.02 us  [body(): lax.all_gather(w_expand, 'dp', axis=0, tiled=True)]
    all_gather x1 -> x0, waiting for transfers between devices: 34.9 us -> none  [body(): key_piece = lax.all_gather(projected[1], 'level', axis=0, tiled=True)]
    concatenate x0 -> x1, other arithmetic: none -> 11.9 us  [body(): jnp.roll(jnp.concatenate([projected[1], lax.ppermute(projected[1], 'level...]
    all_gather x1, waiting for transfers between devices: 29.7 us -> 19.6 us  [body(): lax.all_gather(w_project, 'dp', axis=0, tiled=True)]
  transfers between devices with their start and end apart: 9 -> 9, of which waited for: 6 -> 4; matrix products, arithmetic and copies ran while one was open for 28% -> 32% of each run, Pallas kernels for 0% -> 0%
where the time goes in v1:
time: 372 us; the launch traced here: 371 us
  waiting for transfers between devices  144 us (39%)
  matrix products  96.3 us (26%)
  blocking collectives  54.2 us (15%)
  other arithmetic  42.9 us (12%)
  between operations  14.4 us (4%)
  local copies, waits for them, and re-layouts  12.6 us (3%)
  starting transfers between devices  6.62 us (2%)
    ppermute x1, waiting for transfers between devices, body(): lax.ppermute(projected[1], 'level', [(0, 1), (1, 0)])  64.8 us
    all_gather x1, waiting for transfers between devices, body(): lax.all_gather(final_norm, 'level', axis=0, tiled=True)  43.8 us
    all_to_all x1, blocking collectives, body(): lax.all_to_all(level_terms, 'level', split_axis=0, concat_axis=0, tiled=T...  38.4 us
    dot_general x1, matrix products, body(): jnp.einsum('qhd,khd->hqk', queries, key_three, preferred_element_type=jnp...  28 us
    dot_general x1, matrix products, body(): jnp.einsum('hqk,khd->qhd', weights.astype(jnp.bfloat16), value_three, pre...  27.9 us
    reduce_sum x1, other arithmetic, body(): weight_sum = jnp.sum(weights, axis=-1)  24.5 us
    all_gather x1, waiting for transfers between devices, body(): lax.all_gather(w_project, 'dp', axis=0, tiled=True)  19.6 us
    all_gather x1, waiting for transfers between devices, body(): lax.all_gather(full_columns, 'dp', axis=1, tiled=True)  15.3 us
  transfers between devices with their start and end apart: 9, of which 4 were waited for; matrix products, arithmetic and copies ran while one was open for 32% of the time, Pallas kernels for 0%

profile of v1, /device:TPU:0, one launch (start us, length us, event | category | flops | bytes accessed | tf_op | source)
XLA Modules:
  0.0 371.0 jit_solution(14474659298602656158)
XLA Ops:
  6.5 10.6 %all_gather.24 = bf16[3,64,1024]{2,1,0:T(8,128)(2,1)} all-gather(bf16[3,64,512]{2,1,0:T(8,128)(2,1)} %param.16), channel_id=1, replica_groups=mesh['dp'=16,'level'=2] {'level'}, dimensions={2}, use_global_device_ids=true | all-gather | bytes 589824 | tf_op jit(solution)/shard_map/all_gather | solution.py:75
  17.1 0.0 all-gather.8.cloned.1.call-update
  17.2 0.0 all-gather.18.cloned.1.call-start
  17.9 0.7 broadcast_in_dim.53
  18.6 0.7 reduce.2
  19.3 0.7 or_reduce_fusion
  20.0 4.3 %select_convert_fusion = bf16[1536,1024]{1,0:T(8,128)(2,1)S(1)} fusion(f32[1024]{0:T(1024)S(1)} %bitcast.58, s32[1536]{0:T(1024)S(1)} %reduce.2, pred[1536]{0:T(1024)(128)(4,1)S(1)} %or_reduce_fusion, bf16[1,1024,1024]{2,1,0:T(8,128)(2,1)S(1)} %copy-done), kind=kOutput, calls=%fused_computation.11 | convolution fusion | flops 3224371200 | bytes 5254656 | tf_op jit(solution)/shard_map/dot_general | solution.py:66
  24.3 38.4 %all_to_all.5 = bf16[2,768,1024]{2,1,0:T(8,128)(2,1)S(1)} all-to-all(bf16[2,768,1024]{2,1,0:T(8,128)(2,1)S(1)} %bitcast.50), channel_id=1, replica_groups=mesh['dp'=16,'level'=2] {'level'}, dimensions={0} | all-to-all | bytes 6291456 | tf_op jit(solution)/shard_map/all_to_all | solution.py:72
  62.7 0.7 convert_reduce_fusion
  63.4 0.4 multiply_reduce_fusion.3
  63.8 15.3 %all-gather.8.cloned.1.call-done = bf16[3,1024,1024]{2,1,0:T(8,128)(2,1)} async-done(((bf16[3,64,1024]{2,1,0:T(8,128)(2,1)}), bf16[3,1024,1024]{2,1,0:T(8,128)(2,1)}) %all-gather.8.cloned.1.call-update) | async-done | bytes 6291472 | tf_op jit(solution)/shard_map/all_gather | solution.py:77
  79.1 8.3 %convert_bitcast_fusion = bf16[3,768,1024]{2,1,0:T(8,128)(2,1)S(1)} fusion(bf16[3,1024,1024]{2,1,0:T(8,128)(2,1)} %all-gather.8.cloned.1.call-done, f32[768,1024]{1,0:T(8,128)S(1)} %get-tuple-element.6, f32[768]{0:T(1024)S(1)} %add_rsqrt_fusion.2, f32[768]{0:T(1024)S(1)} %broadcast_multiply_fusion.2), kind=kOutput, calls=%fused_computation.14 | convolution fusion | flops 4836556800 | bytes 14161920 | tf_op jit(solution)/shard_map/fk,jkc->jfc/dot_general | solution.py:33
  87.4 0.0 copy-start.5
  87.4 2.3 slice_bitcast_fusion
  89.7 0.0 all-gather.18.cloned.1.call-update
  89.7 0.0 all-gather.10.cloned.1.call-start
  89.8 5.2 %all_gather.27 = bf16[1024,64]{0,1:T(8,128)(2,1)} all-gather(bf16[512,64]{0,1:T(8,128)(2,1)S(1)} %copy-done.5), channel_id=1, replica_groups=mesh['dp'=16,'level'=2] {'level'}, dimensions={0}, use_global_device_ids=true | all-gather | bytes 196608 | tf_op jit(solution)/shard_map/all_gather | solution.py:113
  94.9 0.0 all-gather.10.cloned.1.call-update
  95.0 0.0 all-gather.12.cloned.1.call-start
  95.0 0.5 all-gather.12.cloned.1.call-update
  95.5 0.0 all-gather.14.cloned.1.call-start
  95.6 1.5 collective-permute-start
  97.1 0.0 all-gather.14.cloned.1.call-update
  97.1 0.2 all-gather.16.cloned.1.call-start
  97.4 2.7 copy.14
  100.0 64.8 %collective-permute-done = bf16[768,1024]{1,0:T(8,128)(2,1)S(1)} collective-permute-done((bf16[768,1024]{1,0:T(8,128)(2,1)}, bf16[768,1024]{1,0:T(8,128)(2,1)S(1)}, u32[]{:S(2)}, u32[]{:S(2)}) %collective-permute-start) | collective-permute-done | bytes 1572896 | tf_op jit(solution)/shard_map/ppermute | solution.py:84
  164.8 11.9 %fusion.8 = bf16[1536,1024]{1,0:T(8,128)(2,1)} fusion(s32[]{:T(128)S(6)} %select_n.19, bf16[768,1024]{1,0:T(8,128)(2,1)S(1)} %copy-done.3, bf16[768,1024]{1,0:T(8,128)(2,1)S(1)} %collective-permute-done), kind=kLoop, calls=%fused_computation.19 | loop fusion | flops 12582912 | bytes 6291460 | tf_op jit(solution)/shard_map/jit(_roll_dynamic)/concatenate | solution.py:82
  176.7 3.2 copy.15
  179.9 28.0 %multiply_reduce_fusion = (f32[16,768]{1,0:T(8,128)S(1)}, f32[16,768,1536]{2,1,0:T(8,128)}) fusion(bf16[768,16,64]{0,2,1:T(8,128)(2,1)} %bitcast.49, bf16[1536,16,64]{0,2,1:T(8,128)(2,1)S(1)} %bitcast.47), kind=kOutput, calls=%fused_computation.1 | convolution fusion | flops 2453655552 | bytes 80265216 | tf_op jit(solution)/shard_map/qhd,khd->hqk/dot_general | solution.py:94
  207.9 24.5 %fusion = f32[16,768]{1,0:T(8,128)S(1)} fusion(f32[16,768,1536]{2,1,0:T(8,128)} %get-tuple-element.20, f32[16,768]{1,0:T(8,128)S(1)} %get-tuple-element.13), kind=kLoop, calls=%fused_computation.2 | loop fusion | flops 56610816 | bytes 75595776 | tf_op jit(solution)/shard_map/reduce_sum | solution.py:99
  232.4 0.0 all-gather.18.cloned.1.call-done
  232.4 3.3 copy.16
  235.7 27.9 %fusion.14 = bf16[768,16,64]{0,2,1:T(8,128)(2,1)} fusion(bf16[1536,16,64]{0,2,1:T(8,128)(2,1)S(1)} %bitcast.48, f32[16,768,1536]{2,1,0:T(8,128)} %get-tuple-element.20, f32[16,768]{1,0:T(8,128)S(1)} %get-tuple-element.13, f32[768,16]{0,1:T(8,128)S(1)} %bitcast.52, f32[768,16]{0,1:T(8,128)S(1)} %get-tuple-element.12), kind=kOutput, calls=%fused_computation.27 | convolution fusion | flops 2474901504 | bytes 80363520 | tf_op jit(solution)/shard_map/hqk,khd->qhd/dot_general | solution.py:100
  263.7 4.9 %fusion.40 = (f32[768]{0:T(1024)S(1)}, f32[768,1024]{1,0:T(8,128)S(1)}) fusion(f32[768,1024]{1,0:T(8,128)} %copy-done.2, bf16[768,1024]{0,1:T(8,128)(2,1)} %bitcast.51, bf16[1024,1024]{0,1:T(8,128)(2,1)} %all-gather.10.cloned.1.call-done), kind=kOutput, calls=%fused_computation.80 | convolution fusion | flops 1612184832 | bytes 9964544 | tf_op jit(solution)/shard_map/dot_general | solution.py:114
  268.6 0.4 multiply_reduce_fusion.2
  269.1 0.0 all-gather.12.cloned.1.call-done
  269.1 5.3 %fusion.25 = f32[768,2048]{1,0:T(8,128)S(1)} fusion(bf16[1024,2048]{1,0:T(8,128)(2,1)} %all-gather.12.cloned.1.call-done, f32[768,1024]{1,0:T(8,128)S(1)} %get-tuple-element.22, f32[768]{0:T(1024)S(1)} %add_rsqrt_fusion.1, f32[768]{0:T(1024)S(1)} %broadcast_multiply_fusion.1), kind=kOutput, calls=%fused_computation.48 | convolution fusion | flops 3223584768 | bytes 13637632 | tf_op jit(solution)/shard_map/dot_general | solution.py:29
  274.5 0.9 fusion.16
  275.3 1.1 copy-done.4
  276.5 3.4 collective-permute-start.1
  279.9 1.3 collective-permute-start.2
  281.2 19.6 %all-gather.14.cloned.1.call-done = bf16[1024,1024]{1,0:T(8,128)(2,1)} async-done(((bf16[64,1024]{1,0:T(8,128)(2,1)}), bf16[1024,1024]{1,0:T(8,128)(2,1)}) %all-gather.14.cloned.1.call-update) | async-done | bytes 2097168 | tf_op jit(solution)/shard_map/all_gather | solution.py:133
  300.8 9.7 %fusion.41 = (f32[768]{0:T(1024)S(1)}, f32[768,1024]{1,0:T(8,128)S(1)}) fusion(f32[768,1024]{1,0:T(8,128)S(1)} %get-tuple-element.22, bf16[1024,1024]{1,0:T(8,128)(2,1)} %all-gather.14.cloned.1.call-done, bf16[768,1024]{1,0:T(8,128)(2,1)} %copy-done.4, bf16[2,1024]{1,0:T(2,128)(2,1)S(1)} %collective-permute-done.2, ...), kind=kOutput, calls=%fused_computation.81 | convolution fusion | flops 1636564224 | bytes 9993216 | tf_op jit(solution)/shard_map/dot_general | solution.py:29
  310.5 0.4 multiply_reduce_fusion.1
  311.0 1.5 multiply_convert_fusion
  312.5 0.0 all-gather.16.cloned.1.call-update
  312.5 43.8 %all-gather.16.cloned.1.call-done = bf16[1536,1024]{1,0:T(8,128)(2,1)} async-done(((bf16[768,1024]{1,0:T(8,128)(2,1)}), bf16[1536,1024]{1,0:T(8,128)(2,1)}) %all-gather.16.cloned.1.call-update) | async-done | bytes 3145744 | tf_op jit(solution)/shard_map/all_gather | solution.py:138
  356.3 7.8 %fusion.5 = bf16[1,1,1536,1024]{3,2,1,0:T(8,128)(2,1)} fusion(bf16[1536,1024]{1,0:T(8,128)(2,1)} %all-gather.16.cloned.1.call-done, bf16[1,1024,1024]{2,1,0:T(8,128)(2,1)} %param.21), kind=kOutput, calls=%fused_computation.16 | convolution fusion | flops 3222798336 | bytes 8388608 | tf_op jit(solution)/shard_map/dot_general | solution.py:137
  (25 shorter events, 0.1 us)
Async XLA Ops:
  6.5 13.5 %copy-start = (bf16[1,1024,1024]{2,1,0:T(8,128)(2,1)S(1)}, bf16[1,1024,1024]{2,1,0:T(8,128)(2,1)}, u32[]{:S(2)}) copy-start(bf16[1,1024,1024]{2,1,0:T(8,128)(2,1)} %param.14) | copy-start | bytes 6291460
  6.5 72.5 %all-gather.8.cloned.1.call-start = ((), (), s32[]{:S(2)}) async-start(), calls=%async_computation.1 | async-start | bytes 6684672 | tf_op jit(solution)/shard_map/all_gather | solution.py:77
  17.2 215.3 %all-gather.18.cloned.1.call-start = ((), (), s32[]{:S(2)}) async-start(), calls=%async_computation.6 | async-start | bytes 4718592 | tf_op jit(solution)/shard_map/all_gather | solution.py:89
  63.3 24.0 %copy-start.2 = (f32[768,1024]{1,0:T(8,128)}, f32[768,1024]{1,0:T(8,128)S(1)}, u32[]{:S(2)}) copy-start(f32[768,1024]{1,0:T(8,128)S(1)} %get-tuple-element.6) | copy-start | bytes 9437188
  87.4 2.4 copy-start.5
  89.7 75.2 %copy-start.3 = (bf16[768,1024]{1,0:T(8,128)(2,1)S(1)}, bf16[768,1024]{1,0:T(8,128)(2,1)}, u32[]{:S(2)}) copy-start(bf16[768,1024]{1,0:T(8,128)(2,1)} %get-tuple-element.7) | copy-start | bytes 4718596
  89.7 174.0 %all-gather.10.cloned.1.call-start = ((), (), s32[]{:S(2)}) async-start(), calls=%async_computation.2 | async-start | bytes 2228224 | tf_op jit(solution)/shard_map/all_gather | solution.py:116
  95.0 174.2 %all-gather.12.cloned.1.call-start = ((), (), s32[]{:S(2)}) async-start(), calls=%async_computation.3 | async-start | bytes 4456448 | tf_op jit(solution)/shard_map/all_gather | solution.py:120
  95.5 205.3 %all-gather.14.cloned.1.call-start = ((), (), s32[]{:S(2)}) async-start(), calls=%async_computation.4 | async-start | bytes 2228224 | tf_op jit(solution)/shard_map/all_gather | solution.py:133
  95.6 69.2 %collective-permute-start = (bf16[768,1024]{1,0:T(8,128)(2,1)}, bf16[768,1024]{1,0:T(8,128)(2,1)S(1)}, u32[]{:S(2)}, u32[]{:S(2)}) collective-permute-start(bf16[768,1024]{1,0:T(8,128)(2,1)} %get-tuple-element.7), channel_id=1, source_target_pairs={{0,1},{1,0},{2,3},{3,2},{4,5},{5,4},{6,7},{7,6},{8,9},{9,8},{10,11... | collective-permute-start | bytes 4718600 | tf_op jit(solution)/shard_map/ppermute | solution.py:84
  97.1 259.2 %all-gather.16.cloned.1.call-start = ((), (), s32[]{:S(2)}) async-start(), calls=%async_computation.5 | async-start | bytes 4718592 | tf_op jit(solution)/shard_map/all_gather | solution.py:138
  274.4 6.8 %copy-start.6 = (bf16[5,1024]{1,0:T(8,128)(2,1)S(1)}, bf16[5,1024]{1,0:T(8,128)(2,1)}, u32[]{:S(2)}) copy-start(bf16[5,1024]{1,0:T(8,128)(2,1)} %param.19) | copy-start | bytes 30724
  275.3 1.1 copy-start.4
  276.5 24.3 %collective-permute-start.1 = (bf16[2,1024]{1,0:T(2,128)(2,1)S(1)}, bf16[2,1024]{1,0:T(2,128)(2,1)S(1)}, u32[]{:S(2)}, u32[]{:S(2)}) collective-permute-start(bf16[2,1024]{1,0:T(2,128)(2,1)S(1)} %get-tuple-element.10), channel_id=1, source_target_pairs={{0,1},{2,3},{4,5},{6,7},{8,9},{10,11},{12,13},{14,15},{16,17},{18,... | collective-permute-start | bytes 12296 | tf_op jit(solution)/shard_map/ppermute | solution.py:16
  279.9 20.9 %collective-permute-start.2 = (bf16[2,1024]{1,0:T(2,128)(2,1)S(1)}, bf16[2,1024]{1,0:T(2,128)(2,1)S(1)}, u32[]{:S(2)}, u32[]{:S(2)}) collective-permute-start(bf16[2,1024]{1,0:T(2,128)(2,1)S(1)} %get-tuple-element.11), channel_id=1, source_target_pairs={{1,0},{3,2},{5,4},{7,6},{9,8},{11,10},{13,12},{15,14},{17,16},{19,... | collective-permute-start | bytes 12296 | tf_op jit(solution)/shard_map/ppermute | solution.py:17
  356.3 7.8 %copy-start.1 = (bf16[1,1024,1024]{2,1,0:T(8,128)(2,1)S(1)}, bf16[1,1024,1024]{2,1,0:T(8,128)(2,1)}, u32[]{:S(2)}) copy-start(bf16[1,1024,1024]{2,1,0:T(8,128)(2,1)} %param.14) | copy-start | bytes 6291460
Sparse Core Ops, SparseCore 0:
  17.3 61.7 all-gather.7
  89.8 75.3 all-gather.17
  167.4 40.1 all-gather.9
  209.6 49.0 all-gather.11
  260.7 40.0 all-gather.13
  312.7 43.6 all-gather.15
